TPU v7x, 32 devices: a whole 2x2x4 slice. The times are simulated.
32 devices in a mesh: shard: 4 (over y, x), rep: 8 (over z, core).
Axes of the slice: x: 2, y: 2, z: 4, core: 2. Of those that a mesh axis runs over, the one named last changes fastest.
Arguments:
- activations: bfloat16 [8, 512, 2048], P('rep', 'shard'), may hold values from -16 to 16
- segments: int32 [8, 512], P('rep'), may hold values from 0 to 3, never falling along the last dimension, each value on 1 to 256 neighbouring positions
- attn_gain: float32 [2048], replicated, may hold values from 0.25 to 1.75
- query_weight: bfloat16 [2048, 2048], P('shard'), may hold values from -0.125 to 0.125
- key_weight: bfloat16 [2048, 1024], P('shard'), may hold values from -0.125 to 0.125
- value_weight: bfloat16 [2048, 1024], P('shard'), may hold values from -0.125 to 0.125
- query_gain: float32 [128], replicated, may hold values from 0.5 to 5.5
- key_gain: float32 [128], replicated, may hold values from 0.5 to 5.5
- out_weight: bfloat16 [2048, 2048], P('shard'), may hold values from -0.75 to 0.75
- mlp_gain: float32 [2048], replicated, may hold values from 0.25 to 1.75
- gate_weight: bfloat16 [2048, 6144], P('shard'), may hold values from -0.125 to 0.125
- up_weight: bfloat16 [2048, 6144], P('shard'), may hold values from -0.125 to 0.125
- down_weight: bfloat16 [6144, 2048], P('shard'), may hold values from -0.078125 to 0.078125
- cotangent: bfloat16 [8, 512, 2048], P('rep', 'shard'), may hold values from -11.1 to 11.1
Outputs:
- output: bfloat16 [8, 512, 2048], P('rep', 'shard')
- grad_input: float32 [8, 512, 2048], P('rep', 'shard')
- grad_attn_gain: float32 [2048], replicated
- grad_query_weight: float32 [2048, 2048], P('shard')
- grad_key_weight: float32 [2048, 1024], P('shard')
- grad_value_weight: float32 [2048, 1024], P('shard')
- grad_query_gain: float32 [128], replicated
- grad_key_gain: float32 [128], replicated
- grad_out_weight: float32 [2048, 2048], P('shard')
- grad_mlp_gain: float32 [2048], replicated
- grad_gate_weight: float32 [2048, 6144], P('shard')
- grad_up_weight: float32 [2048, 6144], P('shard')
- grad_down_weight: float32 [6144, 2048], P('shard')
Inputs may be any that keep to these rules, and one draw needn't show every extreme that they name: `segments`: within each sequence the document numbers never fall; each document has 1 to 256 tokens, and one has exactly 256.
All inputs are finite; a program needn't handle non-finite values.
Results may differ from a plain program's by a relative error of at most 0.02.
The roundings to bfloat16 on the way count: a program that leaves them out, or rounds other values in their place, can miss the bound.
Values may be sent and summed in bfloat16 or wider, within the bound.
A program may use at most 384 MiB of HBM per device.

v0:
```python
from functools import partial
import math
import jax
import jax.numpy as jnp
from jax import lax
from jax.sharding import PartitionSpec as P

HQ = 16
HK = 8
HD = 128
FF = 6144
EPSILON = 1e-06
ROPE_BASE = 1000000.0
MASKED = -1e30


def dims_last(left_op, right_op):
    return lax.dot_general(
        left_op, right_op, (((1,), (1,)), ((), ())), preferred_element_type=jnp.float32
    )


def dims_first(left_op, right_op):
    return lax.dot_general(
        left_op, right_op, (((0,), (0,)), ((), ())), preferred_element_type=jnp.float32
    )


def positions(seg_ids):
    token_index = jnp.arange(seg_ids.shape[0], dtype=jnp.int32)
    before = jnp.concatenate([jnp.full((1,), -1, jnp.int32), seg_ids[:-1]])
    starts = lax.cummax(
        jnp.where(seg_ids != before, token_index, jnp.zeros_like(token_index)), axis=0
    )
    return (token_index - starts).astype(jnp.float32)


def rotary(pos_float):
    half_width = HD // 2
    inv_freq = 1.0 / ROPE_BASE ** (jnp.arange(half_width, dtype=jnp.float32) * (2.0 / HD))
    angles = pos_float[:, None] * inv_freq[None, :]
    return (jnp.cos(angles), jnp.sin(angles))


def rotate(values_in, cosine, sine_part):
    half_width = values_in.shape[-1] // 2
    first_half = values_in[..., :half_width]
    second_half = values_in[..., half_width:]
    cos_b = cosine[:, None, :]
    sin_b = sine_part[:, None, :]
    return jnp.concatenate(
        [first_half * cos_b - second_half * sin_b, second_half * cos_b + first_half * sin_b], -1
    )


def rotate_back(grads_in, cosine, sine_part):
    half_width = grads_in.shape[-1] // 2
    first_half = grads_in[..., :half_width]
    second_half = grads_in[..., half_width:]
    cos_b = cosine[:, None, :]
    sin_b = sine_part[:, None, :]
    return jnp.concatenate(
        [first_half * cos_b + second_half * sin_b, second_half * cos_b - first_half * sin_b], -1
    )


def norm_back(grad_normed, values_in, rstat, gain_vec):
    scaled = values_in * rstat
    lead_axes = tuple(range(grad_normed.ndim - 1))
    grad_gain = jnp.sum(grad_normed * scaled, axis=lead_axes)
    weighted = grad_normed * gain_vec
    grad_values = rstat * (weighted - scaled * jnp.mean(weighted * scaled, -1, keepdims=True))
    return (grad_values, grad_gain)


def head_scores(query_group, key_block, visible, score_scale):
    scores = (
        jnp.einsum("qgd,kd->gqk", query_group, key_block, preferred_element_type=jnp.float32)
        * score_scale
    )
    return jnp.where(visible[None], scores, MASKED)


def attend(head_item, visible, score_scale):
    query_group, key_block, value_block = head_item
    scores = head_scores(query_group, key_block, visible, score_scale)
    row_max = jnp.max(scores, -1, keepdims=True)
    exp_scores = jnp.exp(scores - row_max)
    row_total = jnp.sum(exp_scores, -1, keepdims=True)
    softmax_out = (exp_scores / row_total).astype(jnp.bfloat16)
    head_out = jnp.einsum(
        "gqk,kd->qgd", softmax_out, value_block, preferred_element_type=jnp.float32
    )
    return (head_out, row_max + jnp.log(row_total))


def attend_back(head_item, visible, score_scale):
    query_group, key_block, value_block, grad_head, log_total = head_item
    scores = head_scores(query_group, key_block, visible, score_scale)
    softmax_out = jnp.exp(scores - log_total)
    grad_soft = jnp.einsum(
        "qgd,kd->gqk", grad_head, value_block, preferred_element_type=jnp.float32
    )
    row_delta = jnp.sum(softmax_out * grad_soft, -1, keepdims=True)
    grad_scores = (softmax_out * (grad_soft - row_delta)).astype(jnp.bfloat16)
    grad_group = (
        jnp.einsum("gqk,kd->qgd", grad_scores, key_block, preferred_element_type=jnp.float32)
        * score_scale
    )
    grad_key = (
        jnp.einsum("gqk,qgd->kd", grad_scores, query_group, preferred_element_type=jnp.float32)
        * score_scale
    )
    grad_value = jnp.einsum(
        "gqk,qgd->kd",
        softmax_out.astype(jnp.bfloat16),
        grad_head,
        preferred_element_type=jnp.float32,
    )
    return (grad_group, grad_key, grad_value)


def per_device(
    activations,
    segments,
    attn_gain,
    query_weight,
    key_weight,
    value_weight,
    query_gain,
    key_gain,
    out_weight,
    mlp_gain,
    gate_weight,
    up_weight,
    down_weight,
    cotangent,
):
    tok_rows = activations.shape[1]
    length = segments.shape[1]
    groups = HQ // HK
    score_scale = 1.0 / math.sqrt(HD)
    offset = lax.axis_index("shard") * tok_rows
    seg_ids = segments[0]
    pos_float = lax.dynamic_slice_in_dim(positions(seg_ids), offset, tok_rows)
    cosine, sine_part = rotary(pos_float)
    key_index = jnp.arange(length, dtype=jnp.int32)
    query_rows = offset + jnp.arange(tok_rows, dtype=jnp.int32)
    seg_rows = lax.dynamic_slice_in_dim(seg_ids, offset, tok_rows)
    visible = (key_index[None, :] <= query_rows[:, None]) & (seg_ids[None, :] == seg_rows[:, None])
    inputs = activations[0].astype(jnp.float32)
    rstat_attn = lax.rsqrt(jnp.mean(inputs * inputs, -1, keepdims=True) + EPSILON)
    normed = (inputs * rstat_attn * attn_gain).astype(jnp.bfloat16)
    full_query, full_key, full_value, full_out = (
        lax.all_gather(query_weight, "shard", axis=0, tiled=True),
        lax.all_gather(key_weight, "shard", axis=0, tiled=True),
        lax.all_gather(value_weight, "shard", axis=0, tiled=True),
        lax.all_gather(out_weight, "shard", axis=0, tiled=True),
    )
    queries = jnp.dot(normed, full_query, preferred_element_type=jnp.float32).reshape(
        tok_rows, HQ, HD
    )
    keys_raw = jnp.dot(normed, full_key, preferred_element_type=jnp.float32).reshape(
        tok_rows, HK, HD
    )
    values_low = jnp.dot(normed, full_value, preferred_element_type=jnp.float32).astype(
        jnp.bfloat16
    )
    query_rstat = lax.rsqrt(jnp.mean(queries * queries, -1, keepdims=True) + EPSILON)
    key_rstat = lax.rsqrt(jnp.mean(keys_raw * keys_raw, -1, keepdims=True) + EPSILON)
    query_rot = rotate(queries * query_rstat * query_gain, cosine, sine_part).astype(jnp.bfloat16)
    key_rot = rotate(keys_raw * key_rstat * key_gain, cosine, sine_part).astype(jnp.bfloat16)
    key_heads = jnp.transpose(key_rot, (1, 0, 2))
    value_heads = jnp.transpose(values_low.reshape(tok_rows, HK, HD), (1, 0, 2))
    all_keys, all_values = (
        lax.all_gather(key_heads, "shard", axis=1, tiled=True),
        lax.all_gather(value_heads, "shard", axis=1, tiled=True),
    )
    query_heads = jnp.transpose(query_rot.reshape(tok_rows, HK, groups, HD), (1, 0, 2, 3))
    attn_heads, log_totals = lax.map(
        partial(attend, visible=visible, score_scale=score_scale),
        (query_heads, all_keys, all_values),
    )
    attn_out = (
        jnp.transpose(attn_heads, (1, 0, 2, 3)).reshape(tok_rows, HQ * HD).astype(jnp.bfloat16)
    )
    hidden = inputs + jnp.dot(attn_out, full_out, preferred_element_type=jnp.float32)
    rstat_mlp = lax.rsqrt(jnp.mean(hidden * hidden, -1, keepdims=True) + EPSILON)
    normed_mlp = (hidden * rstat_mlp * mlp_gain).astype(jnp.bfloat16)
    full_gate, full_up, full_down = (
        lax.all_gather(gate_weight, "shard", axis=0, tiled=True),
        lax.all_gather(up_weight, "shard", axis=0, tiled=True),
        lax.all_gather(down_weight, "shard", axis=0, tiled=True),
    )
    gate_pre = jnp.dot(normed_mlp, full_gate, preferred_element_type=jnp.float32)
    up_pre = jnp.dot(normed_mlp, full_up, preferred_element_type=jnp.float32)
    sigmoid_gate = jax.nn.sigmoid(gate_pre)
    activated = (gate_pre * sigmoid_gate * up_pre).astype(jnp.bfloat16)
    result = hidden + jnp.dot(activated, full_down, preferred_element_type=jnp.float32)
    output = result.astype(jnp.bfloat16)[None]
    grad_out = cotangent[0]
    back_gate, back_up, back_down = (
        lax.all_gather(gate_weight, "shard", axis=0, tiled=True),
        lax.all_gather(up_weight, "shard", axis=0, tiled=True),
        lax.all_gather(down_weight, "shard", axis=0, tiled=True),
    )
    grad_act = dims_last(grad_out, back_down)
    grad_gate = (grad_act * up_pre * sigmoid_gate * (1.0 + gate_pre * (1.0 - sigmoid_gate))).astype(
        jnp.bfloat16
    )
    grad_up = (grad_act * gate_pre * sigmoid_gate).astype(jnp.bfloat16)
    grad_normed_mlp = dims_last(grad_gate, back_gate) + dims_last(grad_up, back_up)
    grad_hidden_part, grad_mlp_gain = norm_back(grad_normed_mlp, hidden, rstat_mlp, mlp_gain)
    grad_hidden = grad_out.astype(jnp.float32) + grad_hidden_part
    grad_branch = grad_hidden.astype(jnp.bfloat16)
    back_query, back_key, back_value, back_out = (
        lax.all_gather(query_weight, "shard", axis=0, tiled=True),
        lax.all_gather(key_weight, "shard", axis=0, tiled=True),
        lax.all_gather(value_weight, "shard", axis=0, tiled=True),
        lax.all_gather(out_weight, "shard", axis=0, tiled=True),
    )
    grad_attn = dims_last(grad_branch, back_out).astype(jnp.bfloat16)
    grad_heads = jnp.transpose(grad_attn.reshape(tok_rows, HK, groups, HD), (1, 0, 2, 3))
    grad_query_heads, grad_keys_all, grad_values_all = lax.map(
        partial(attend_back, visible=visible, score_scale=score_scale),
        (query_heads, all_keys, all_values, grad_heads, log_totals),
    )
    own_keys, own_values = (
        lax.psum_scatter(
            grad_keys_all.astype(jnp.bfloat16), "shard", scatter_dimension=1, tiled=True
        ).astype(jnp.float32),
        lax.psum_scatter(
            grad_values_all.astype(jnp.bfloat16), "shard", scatter_dimension=1, tiled=True
        ).astype(jnp.float32),
    )
    grad_query_rot = jnp.transpose(grad_query_heads, (1, 0, 2, 3)).reshape(tok_rows, HQ, HD)
    grad_key_rot = jnp.transpose(own_keys, (1, 0, 2))
    grad_value = (
        jnp.transpose(own_values, (1, 0, 2)).reshape(tok_rows, HK * HD).astype(jnp.bfloat16)
    )
    grad_query_norm, grad_query_gain = norm_back(
        rotate_back(grad_query_rot, cosine, sine_part), queries, query_rstat, query_gain
    )
    grad_key_norm, grad_key_gain = norm_back(
        rotate_back(grad_key_rot, cosine, sine_part), keys_raw, key_rstat, key_gain
    )
    grad_query = grad_query_norm.reshape(tok_rows, HQ * HD).astype(jnp.bfloat16)
    grad_key = grad_key_norm.reshape(tok_rows, HK * HD).astype(jnp.bfloat16)
    grad_normed = (
        dims_last(grad_query, back_query)
        + dims_last(grad_key, back_key)
        + dims_last(grad_value, back_value)
    )
    grad_input_part, grad_attn_gain = norm_back(grad_normed, inputs, rstat_attn, attn_gain)
    grad_input = (grad_hidden + grad_input_part)[None]
    grad_attn_gain, grad_query_gain, grad_key_gain, grad_mlp_gain = lax.psum(
        (grad_attn_gain, grad_query_gain, grad_key_gain, grad_mlp_gain), ("shard", "rep")
    )
    grad_qkv = jnp.concatenate([grad_query, grad_key, grad_value], 1)
    grad_mlp = jnp.concatenate([grad_gate, grad_up], 1)
    cols_attn, cols_mlp, cols_heads, cols_act = (
        lax.all_to_all(normed, "shard", split_axis=1, concat_axis=0, tiled=True),
        lax.all_to_all(normed_mlp, "shard", split_axis=1, concat_axis=0, tiled=True),
        lax.all_to_all(attn_out, "shard", split_axis=1, concat_axis=0, tiled=True),
        lax.all_to_all(activated, "shard", split_axis=1, concat_axis=0, tiled=True),
    )
    piece_qkv = lax.all_gather(grad_qkv, "shard", axis=0, tiled=True)
    piece_mlp = lax.all_gather(grad_mlp, "shard", axis=0, tiled=True)
    piece_branch = lax.all_gather(grad_branch, "shard", axis=0, tiled=True)
    piece_out = lax.all_gather(grad_out, "shard", axis=0, tiled=True)
    added_in = jnp.concatenate(
        [dims_first(cols_attn, piece_qkv), dims_first(cols_mlp, piece_mlp)], 1
    )
    part_out = dims_first(cols_heads, piece_branch)
    part_down = dims_first(cols_act, piece_out)
    owned_in, owned_out, owned_down = (
        lax.psum(added_in.astype(jnp.bfloat16), "rep").astype(jnp.float32),
        lax.psum(part_out.astype(jnp.bfloat16), "rep").astype(jnp.float32),
        lax.psum(part_down.astype(jnp.bfloat16), "rep").astype(jnp.float32),
    )
    width_query = HQ * HD
    width_kv = HK * HD
    edge_key = width_query + width_kv
    edge_value = edge_key + width_kv
    edge_gate = edge_value + FF
    grad_query_weight = owned_in[:, :width_query]
    grad_key_weight = owned_in[:, width_query:edge_key]
    grad_value_weight = owned_in[:, edge_key:edge_value]
    grad_gate_weight = owned_in[:, edge_value:edge_gate]
    grad_up_weight = owned_in[:, edge_gate:]
    return (
        output,
        grad_input,
        grad_attn_gain,
        grad_query_weight,
        grad_key_weight,
        grad_value_weight,
        grad_query_gain,
        grad_key_gain,
        owned_out,
        grad_mlp_gain,
        grad_gate_weight,
        grad_up_weight,
        owned_down,
    )


def solution(mesh):
    placed = (
        P("rep", "shard", None),
        P("rep", None),
        P(),
        P("shard", None),
        P("shard", None),
        P("shard", None),
        P(),
        P(),
        P("shard", None),
        P(),
        P("shard", None),
        P("shard", None),
        P("shard", None),
        P("rep", "shard", None),
    )
    return jax.shard_map(
        per_device,
        mesh=mesh,
        in_specs=placed,
        out_specs=(
            P("rep", "shard", None),
            P("rep", "shard", None),
            P(),
            P("shard", None),
            P("shard", None),
            P("shard", None),
            P(),
            P(),
            P("shard", None),
            P(),
            P("shard", None),
            P("shard", None),
            P("shard", None),
        ),
        check_vma=False,
    )
```

profile of v0, /device:TPU:0, one launch (start us, length us, event | category | flops | bytes accessed | tf_op | source)
XLA Modules:
  0.0 2083.6 jit_solution(7904533563809124515)
XLA Ops:
  11.7 53.4 %all-gather.19.cloned.1.call-done = bf16[2048,1024]{1,0:T(8,128)(2,1)} async-done(((bf16[512,1024]{1,0:T(8,128)(2,1)}), bf16[2048,1024]{1,0:T(8,128)(2,1)}) %all-gather.19.cloned.1.call-update) | async-done | bytes 4194320 | tf_op jit(solution)/shard_map/all_gather | solution.py:156
  77.7 41.9 %all-gather.15.cloned.1.call-done = bf16[2048,1024]{1,0:T(8,128)(2,1)} async-done(((bf16[512,1024]{1,0:T(8,128)(2,1)}), bf16[2048,1024]{1,0:T(8,128)(2,1)}) %all-gather.15.cloned.1.call-update) | async-done | bytes 4194320 | tf_op jit(solution)/shard_map/all_gather | solution.py:157
  128.3 20.1 all-gather.21.cloned.1.call-done
  150.0 87.6 %all-gather.23.cloned.1.call-done = bf16[2048,2048]{1,0:T(8,128)(2,1)} async-done(((bf16[512,2048]{1,0:T(8,128)(2,1)}), bf16[2048,2048]{1,0:T(8,128)(2,1)}) %all-gather.23.cloned.1.call-update) | async-done | bytes 8388624 | tf_op jit(solution)/shard_map/all_gather | solution.py:155
  266.4 28.7 %while.30 = (s32[]{:T(128)}, bf16[8,128,2,128]{1,3,2,0:T(8,128)(2,1)}, f32[8,2,128,1]{2,1,3,0:T(2,128)}, bf16[8,512,128]{2,1,0:T(8,128)(2,1)}, bf16[8,512,128]{2...) while((s32[]{:T(128)}, ...), condition=%wide.region_8.9_spmd.clone.clone, body=%wide.region_5.8_spmd.clone.sunk.clone | while | flops 68353792 | bytes 2176605 | solution.py:180
  295.1 60.5 %all-gather.25.cloned.1.call-done = bf16[2048,2048]{1,0:T(8,128)(2,1)} async-done(((bf16[512,2048]{1,0:T(8,128)(2,1)}), bf16[2048,2048]{1,0:T(8,128)(2,1)}) %all-gather.25.cloned.1.call-update) | async-done | bytes 8388624 | tf_op jit(solution)/shard_map/all_gather | solution.py:158
  360.8 224.3 %all-gather.27.cloned.1.call-done = bf16[2048,6144]{1,0:T(8,128)(2,1)} async-done(((bf16[512,6144]{1,0:T(8,128)(2,1)}), bf16[2048,6144]{1,0:T(8,128)(2,1)}) %all-gather.27.cloned.1.call-update) | async-done | bytes 25165840 | tf_op jit(solution)/shard_map/all_gather | solution.py:191
  585.1 13.7 fusion.86
  598.8 215.8 %all-gather.29.cloned.1.call-done = bf16[2048,6144]{1,0:T(8,128)(2,1)} async-done(((bf16[512,6144]{1,0:T(8,128)(2,1)}), bf16[2048,6144]{1,0:T(8,128)(2,1)}) %all-gather.29.cloned.1.call-update) | async-done | bytes 25165840 | tf_op jit(solution)/shard_map/all_gather | solution.py:192
  814.6 13.7 fusion.87
  828.3 215.8 %all-gather.31.cloned.1.call-done = bf16[6144,2048]{1,0:T(8,128)(2,1)} async-done(((bf16[1536,2048]{1,0:T(8,128)(2,1)}), bf16[6144,2048]{1,0:T(8,128)(2,1)}) %all-gather.31.cloned.1.call-update) | async-done | bytes 25165840 | tf_op jit(solution)/shard_map/all_gather | solution.py:193
  1044.1 16.8 multiply_convert_fusion.1
  1060.9 14.5 fusion.88
  1075.4 15.3 multiply_reduce_fusion.1
  1102.7 86.9 %while.31 = (s32[]{:T(128)}, f32[8,128,2,128]{1,3,2,0:T(8,128)}, bf16[8,512,128]{1,2,0:T(8,128)(2,1)}, bf16[8,512,128]{1,2,0:T(8,128)(2,1)}, bf16[8,512,128]{2,1...) while((s32[]{:T(128)}, f32[8,128,2,128]{1,3,2,0:T(8,128)}, ...), condition=%wide.region_13.14_spmd.clone.clone, body=%wide.region_11.13_spmd.clone.sunk.clone | while | flops 169312000 | bytes 5780601 | solution.py:224
  1204.2 18.4 reduce-scatter.7.cloned.1.call-done
  1223.8 30.2 %reduce-scatter.9.cloned.1.call-done = bf16[128,1024]{1,0:T(8,128)(2,1)} async-done(((bf16[512,1024]{1,0:T(8,128)(2,1)}), bf16[128,1024]{1,0:T(8,128)(2,1)}) %reduce-scatter.9.cloned.1.call-update) | async-done | bytes 262160
  1288.6 23.6 %all-to-all-done.3 = bf16[128,4,1536]{2,0,1:T(8,128)(2,1)} async-done(((bf16[128,4,1536]{2,0,1:T(8,128)(2,1)}), bf16[128,4,1536]{2,0,1:T(8,128)(2,1)}, u32[]{:S(2)}, u32[]{:S(2)}) %all-to-all-start.3) | async-done | bytes 1572896 | tf_op jit(solution)/shard_map/all_to_all | solution.py:265
  1324.0 25.4 %all-gather.37.cloned.1.call-done = bf16[512,2048]{1,0:T(8,128)(2,1)} async-done(((bf16[128,2048]{1,0:T(8,128)(2,1)}), bf16[512,2048]{1,0:T(8,128)(2,1)}) %all-gather.37.cloned.1.call-update) | async-done | bytes 2097168 | tf_op jit(solution)/shard_map/all_gather | solution.py:269
  1358.2 49.5 %all-gather.33.cloned.1.call-done = bf16[512,4096]{0,1:T(8,128)(2,1)} async-done(((bf16[128,4096]{0,1:T(8,128)(2,1)}), bf16[512,4096]{0,1:T(8,128)(2,1)}) %all-gather.33.cloned.1.call-update) | async-done | bytes 4194320 | tf_op jit(solution)/shard_map/all_gather | solution.py:267
  1414.5 117.9 %all-gather.35.cloned.1.call-done = bf16[512,12288]{1,0:T(8,128)(2,1)} async-done(((bf16[128,12288]{1,0:T(8,128)(2,1)}), bf16[512,12288]{1,0:T(8,128)(2,1)}) %all-gather.35.cloned.1.call-update) | async-done | bytes 12582928 | tf_op jit(solution)/shard_map/all_gather | solution.py:268
  1575.8 41.9 %all-reduce = (f32[2048]{0:T(1024)}, f32[128]{0:T(128)}, f32[128]{0:T(128)}, f32[2048]{0:T(1024)}) all-reduce(f32[2048]{0:T(1024)S(1)} %get-tuple-element.250, f32[128]{0:T(128)S(1)} %get-tuple-element.246, f32[128]{0:T(128)S(1)} %get-tuple-element.252, f32[2048]{0:T(1024)S(1)} %copy-done.29), channel_id=1, replica_groups=mesh['shard'=4,'rep'=8] {'shard','rep'}, use_global_device_ids=true, to_apply=%region_20.21 | all-reduce | flops 4352 | bytes 34816 | tf_op jit(solution)/shard_map/psum | solution.py:256
  1620.5 424.3 %all-reduce.4.cloned.1.call-done = (bf16[512,16384]{1,0:T(8,128)(2,1)}, bf16[512,2048]{1,0:T(8,128)(2,1)}, bf16[1536,2048]{1,0:T(8,128)(2,1)}) async-done(((bf16[512,16384]{1,0:T(8,128)(2,1)}, bf16[512,2048]{1,0:T(8,128)(2,1)}, bf16[1536,2048]{1,0:T(8,128)(2,1)}), (bf16[512,16384]{1,0:T(8,128)(2,1)}, bf16[512,2048]{1,0:T(8,128)(2,1)}, bf16[1536,2048]{1,0:T(8,128)(2,1)})) %all-reduce.4.cloned.1.call-update) | async-done | bytes 25165840 | tf_op jit(solution)/shard_map/psum | solution.py:277
  2044.9 15.6 fusion.84
  (329 shorter events, 328.0 us)
Async XLA Ops:
  7.2 58.0 %all-gather.19.cloned.1.call-start = ((), (), s32[]{:S(2)}) async-start(), calls=%async_computation.8 | async-start | bytes 5242880 | tf_op jit(solution)/shard_map/all_gather | solution.py:156
  7.9 111.7 %all-gather.15.cloned.1.call-start = ((), (), s32[]{:S(2)}) async-start(), calls=%async_computation.6 | async-start | bytes 5242880 | tf_op jit(solution)/shard_map/all_gather | solution.py:157
  8.7 139.7 %all-gather.21.cloned.1.call-start = ((), (), s32[]{:S(2)}) async-start(), calls=%async_computation.9 | async-start | bytes 1310720 | tf_op jit(solution)/shard_map/all_gather | solution.py:176
  11.7 244.3 %copy-start.18 = (f32[128,64]{0,1:T(8,128)}, f32[128,64]{0,1:T(8,128)S(1)}, u32[]{:S(2)}) copy-start(f32[128,64]{0,1:T(8,128)S(1)} %get-tuple-element.322) | copy-start | bytes 98308
  11.7 244.3 %copy-start.20 = (f32[128,64]{0,1:T(8,128)}, f32[128,64]{0,1:T(8,128)S(1)}, u32[]{:S(2)}) copy-start(f32[128,64]{0,1:T(8,128)S(1)} %get-tuple-element.323) | copy-start | bytes 98308
  77.1 160.5 %all-gather.23.cloned.1.call-start = ((), (), s32[]{:S(2)}) async-start(), calls=%async_computation.10 | async-start | bytes 10485760 | tf_op jit(solution)/shard_map/all_gather | solution.py:155
  77.7 188.7 %all-gather.17.cloned.1.call-start = ((), (), s32[]{:S(2)}) async-start(), calls=%async_computation.7 | async-start | bytes 1310720 | tf_op jit(solution)/shard_map/all_gather | solution.py:177
  123.3 232.3 %all-gather.25.cloned.1.call-start = ((), (), s32[]{:S(2)}) async-start(), calls=%async_computation.11 | async-start | bytes 10485760 | tf_op jit(solution)/shard_map/all_gather | solution.py:158
  123.9 461.2 %all-gather.27.cloned.1.call-start = ((), (), s32[]{:S(2)}) async-start(), calls=%async_computation.12 | async-start | bytes 31457280 | tf_op jit(solution)/shard_map/all_gather | solution.py:191
  124.7 689.9 %all-gather.29.cloned.1.call-start = ((), (), s32[]{:S(2)}) async-start(), calls=%async_computation.13 | async-start | bytes 31457280 | tf_op jit(solution)/shard_map/all_gather | solution.py:192
  125.4 918.6 %all-gather.31.cloned.1.call-start = ((), (), s32[]{:S(2)}) async-start(), calls=%async_computation.14 | async-start | bytes 31457280 | tf_op jit(solution)/shard_map/all_gather | solution.py:193
  126.2 1096.4 %reduce-scatter.7.cloned.1.call-start = ((), (), s32[]{:S(2)}) async-start(), calls=%async_computation.19 | async-start | bytes 1310720
  360.6 730.1 %copy-start.32 = (f32[128]{0:T(128)}, f32[128]{0:T(128)S(1)}, u32[]{:S(2)}) copy-start(f32[128]{0:T(128)S(1)} %add_rsqrt_fusion.2) | copy-start | bytes 1540
  360.8 453.8 %copy-start.4 = (bf16[128,2048]{1,0:T(8,128)(2,1)}, bf16[128,2048]{1,0:T(8,128)(2,1)S(1)}, u32[]{:S(2)}) copy-start(bf16[128,2048]{1,0:T(8,128)(2,1)S(1)} %multiply_convert_fusion.5) | copy-start | bytes 1572868
  1194.5 59.5 %reduce-scatter.9.cloned.1.call-start = ((), (), s32[]{:S(2)}) async-start(), calls=%async_computation.20 | async-start | bytes 1310720
  1199.5 116.3 %all-gather.39.cloned.1.call-start = ((), (), s32[]{:S(2)}) async-start(), calls=%async_computation.18 | async-start | bytes 2621440 | tf_op jit(solution)/shard_map/all_gather | solution.py:270
  1200.1 149.4 %all-gather.37.cloned.1.call-start = ((), (), s32[]{:S(2)}) async-start(), calls=%async_computation.17 | async-start | bytes 2621440 | tf_op jit(solution)/shard_map/all_gather | solution.py:269
  1200.8 206.9 %all-gather.33.cloned.1.call-start = ((), (), s32[]{:S(2)}) async-start(), calls=%async_computation.15 | async-start | bytes 5242880 | tf_op jit(solution)/shard_map/all_gather | solution.py:267
  1256.8 275.6 %all-gather.35.cloned.1.call-start = ((), (), s32[]{:S(2)}) async-start(), calls=%async_computation.16 | async-start | bytes 15728640 | tf_op jit(solution)/shard_map/all_gather | solution.py:268
  1260.7 16.6 all-to-all-start.2
  1277.3 35.0 %all-to-all-start.3 = ((bf16[128,4,1536]{2,0,1:T(8,128)(2,1)}), bf16[128,4,1536]{2,0,1:T(8,128)(2,1)}, u32[]{:S(2)}, u32[]{:S(2)}) async-start(bf16[128,4,1536]{2,0,1:T(8,128)(2,1)} %bitcast.331), calls=%async_computation.3 | async-start | bytes 3145728 | tf_op jit(solution)/shard_map/all_to_all | solution.py:265
  1312.3 41.6 %all-to-all-start = ((bf16[128,4,512]{2,0,1:T(8,128)(2,1)}), bf16[128,4,512]{2,0,1:T(8,128)(2,1)S(1)}, u32[]{:S(2)}, u32[]{:S(2)}) async-start(bf16[128,4,512]{2,0,1:T(8,128)(2,1)} %fusion.56), calls=%async_computation | async-start | bytes 1048576 | tf_op jit(solution)/shard_map/all_to_all | solution.py:262
  1354.6 59.8 %all-to-all-start.1 = ((bf16[128,4,512]{2,0,1:T(8,128)(2,1)}), bf16[128,4,512]{2,0,1:T(8,128)(2,1)S(1)}, u32[]{:S(2)}, u32[]{:S(2)}) async-start(bf16[128,4,512]{2,0,1:T(8,128)(2,1)} %bitcast.345), calls=%async_computation.1 | async-start | bytes 1048576 | tf_op jit(solution)/shard_map/all_to_all | solution.py:263
  1358.1 686.8 %all-reduce.4.cloned.1.call-start = ((), (), s32[]{:S(2)}) async-start(), calls=%async_computation.21 | async-start | bytes 50331648 | tf_op jit(solution)/shard_map/psum | solution.py:277
  (38 other events, 936.6 us)
Sparse Core Ops, SparseCore 0:
  9.8 55.2 all-gather.18
  67.0 52.5 all-gather.14
  122.0 26.3 all-gather.20
  150.1 87.4 all-gather.22
  239.9 26.4 all-gather.16
  268.1 87.4 all-gather.24
  357.5 227.5 all-gather.26
  587.0 227.5 all-gather.28
  816.4 227.5 all-gather.30
  1194.6 27.9 reduce-scatter.6
  1226.0 27.9 reduce-scatter.8
  1255.7 56.7 all-gather.38
  1314.3 35.1 all-gather.36
  1351.7 55.9 all-gather.32
  1410.0 122.3 all-gather.34
  1553.3 491.5 all-reduce.3
where the time goes:
time: 2090 us; the launch traced here: 2080 us
  waiting for transfers between devices  1630 us (78%)
  matrix products  228 us (11%)
  local copies, waits for them, and re-layouts  91.2 us (4%)
  other arithmetic  59.5 us (3%)
  blocking collectives  41.9 us (2%)
    psum x1, waiting for transfers between devices, per_device(): lax.psum(added_in.astype(jnp.bfloat16), 'rep').astype(jnp.float32)  424 us
    all_gather x1, waiting for transfers between devices, per_device(): lax.all_gather(gate_weight, 'shard', axis=0, tiled=True)  224 us
    all_gather x1, waiting for transfers between devices, per_device(): lax.all_gather(down_weight, 'shard', axis=0, tiled=True)  216 us
    all_gather x1, waiting for transfers between devices, per_device(): lax.all_gather(up_weight, 'shard', axis=0, tiled=True)  216 us
    all_gather x1, waiting for transfers between devices, per_device(): piece_mlp = lax.all_gather(grad_mlp, 'shard', axis=0, tiled=True)  118 us
    all_gather x1, waiting for transfers between devices, per_device(): lax.all_gather(query_weight, 'shard', axis=0, tiled=True)  87.6 us
    dot_general x7, matrix products, dims_last(): lax.dot_general(left_op, right_op, (((1,), (1,)), ((), ())), preferred_el...  63.7 us
    all_gather x1, waiting for transfers between devices, per_device(): lax.all_gather(out_weight, 'shard', axis=0, tiled=True)  60.5 us
  transfers between devices with their start and end apart: 20, of which 17 were waited for; matrix products, arithmetic and copies ran while one was open for 8% of the time, Pallas kernels for 0%

commit v1 on v0

--- a/solution.py
+++ b/solution.py
@@ -12,6 +12,7 @@
 EPSILON = 1e-06
 ROPE_BASE = 1000000.0
 MASKED = -1e30
+scan_pipes_by_axis = lambda x_part: lax.all_gather(x_part, "rep").sum(axis=0)
 
 
 def dims_last(left_op, right_op):
@@ -274,7 +275,7 @@
     part_out = dims_first(cols_heads, piece_branch)
     part_down = dims_first(cols_act, piece_out)
     owned_in, owned_out, owned_down = (
-        lax.psum(added_in.astype(jnp.bfloat16), "rep").astype(jnp.float32),
+        scan_pipes_by_axis(added_in.astype(jnp.bfloat16)).astype(jnp.float32),
         lax.psum(part_out.astype(jnp.bfloat16), "rep").astype(jnp.float32),
         lax.psum(part_down.astype(jnp.bfloat16), "rep").astype(jnp.float32),
     )

time: 2090 us -> 2890 us (1.38)
  waiting for transfers between devices: 1630 us -> 2410 us
  other arithmetic: 59.5 us -> 100 us
    all_gather x0 -> x1, waiting for transfers between devices: none -> 1100 us  [lax.all_gather(x_part, 'rep').sum(axis=0)]
    psum x1, waiting for transfers between devices: 424 us -> 94.1 us  [per_device(): lax.psum(part_out.astype(jnp.bfloat16), 'rep').astype(jnp.float32)]
    reduce_sum x0 -> x1, other arithmetic: none -> 50 us  [lax.all_gather(x_part, 'rep').sum(axis=0)]
  transfers between devices with their start and end apart: 20 -> 21, of which waited for: 17 -> 18; matrix products, arithmetic and copies ran while one was open for 8% -> 7% of each run, Pallas kernels for 0% -> 0%
where the time goes in v1:
time: 2890 us; the launch traced here: 2880 us
  waiting for transfers between devices  2410 us (83%)
  matrix products  227 us (8%)
  other arithmetic  100 us (3%)
  local copies, waits for them, and re-layouts  74 us (3%)
  blocking collectives  41.2 us (1%)
    all_gather x1, waiting for transfers between devices, lax.all_gather(x_part, 'rep').sum(axis=0)  1100 us
    all_gather x1, waiting for transfers between devices, per_device(): lax.all_gather(gate_weight, 'shard', axis=0, tiled=True)  224 us
    all_gather x1, waiting for transfers between devices, per_device(): lax.all_gather(down_weight, 'shard', axis=0, tiled=True)  216 us
    all_gather x1, waiting for transfers between devices, per_device(): lax.all_gather(up_weight, 'shard', axis=0, tiled=True)  216 us
    all_gather x1, waiting for transfers between devices, per_device(): piece_mlp = lax.all_gather(grad_mlp, 'shard', axis=0, tiled=True)  118 us
    psum x1, waiting for transfers between devices, per_device(): lax.psum(part_out.astype(jnp.bfloat16), 'rep').astype(jnp.float32)  94.1 us
    all_gather x1, waiting for transfers between devices, per_device(): lax.all_gather(query_weight, 'shard', axis=0, tiled=True)  87.6 us
    all_gather x1, waiting for transfers between devices, per_device(): lax.all_gather(out_weight, 'shard', axis=0, tiled=True)  63.7 us
  transfers between devices with their start and end apart: 21, of which 18 were waited for; matrix products, arithmetic and copies ran while one was open for 7% of the time, Pallas kernels for 0%

profile of v1, /device:TPU:0, one launch (start us, length us, event | category | flops | bytes accessed | tf_op | source)
XLA Modules:
  0.0 2881.1 jit_solution(2364602055634660010)
XLA Ops:
  11.7 53.5 %all-gather.20.cloned.1.call-done = bf16[2048,1024]{1,0:T(8,128)(2,1)} async-done(((bf16[512,1024]{1,0:T(8,128)(2,1)}), bf16[2048,1024]{1,0:T(8,128)(2,1)}) %all-gather.20.cloned.1.call-update) | async-done | bytes 4194320 | tf_op jit(solution)/shard_map/all_gather | solution.py:157
  77.7 41.9 %all-gather.16.cloned.1.call-done = bf16[2048,1024]{1,0:T(8,128)(2,1)} async-done(((bf16[512,1024]{1,0:T(8,128)(2,1)}), bf16[2048,1024]{1,0:T(8,128)(2,1)}) %all-gather.16.cloned.1.call-update) | async-done | bytes 4194320 | tf_op jit(solution)/shard_map/all_gather | solution.py:158
  127.2 21.2 all-gather.22.cloned.1.call-done
  150.0 87.6 %all-gather.24.cloned.1.call-done = bf16[2048,2048]{1,0:T(8,128)(2,1)} async-done(((bf16[512,2048]{1,0:T(8,128)(2,1)}), bf16[2048,2048]{1,0:T(8,128)(2,1)}) %all-gather.24.cloned.1.call-update) | async-done | bytes 8388624 | tf_op jit(solution)/shard_map/all_gather | solution.py:156
  266.4 25.5 while.30
  292.0 63.7 %all-gather.26.cloned.1.call-done = bf16[2048,2048]{1,0:T(8,128)(2,1)} async-done(((bf16[512,2048]{1,0:T(8,128)(2,1)}), bf16[2048,2048]{1,0:T(8,128)(2,1)}) %all-gather.26.cloned.1.call-update) | async-done | bytes 8388624 | tf_op jit(solution)/shard_map/all_gather | solution.py:159
  360.8 224.3 %all-gather.28.cloned.1.call-done = bf16[2048,6144]{1,0:T(8,128)(2,1)} async-done(((bf16[512,6144]{1,0:T(8,128)(2,1)}), bf16[2048,6144]{1,0:T(8,128)(2,1)}) %all-gather.28.cloned.1.call-update) | async-done | bytes 25165840 | tf_op jit(solution)/shard_map/all_gather | solution.py:192
  598.8 215.8 %all-gather.30.cloned.1.call-done = bf16[2048,6144]{1,0:T(8,128)(2,1)} async-done(((bf16[512,6144]{1,0:T(8,128)(2,1)}), bf16[2048,6144]{1,0:T(8,128)(2,1)}) %all-gather.30.cloned.1.call-update) | async-done | bytes 25165840 | tf_op jit(solution)/shard_map/all_gather | solution.py:193
  814.6 13.7 fusion.89
  828.3 215.8 %all-gather.32.cloned.1.call-done = bf16[6144,2048]{1,0:T(8,128)(2,1)} async-done(((bf16[1536,2048]{1,0:T(8,128)(2,1)}), bf16[6144,2048]{1,0:T(8,128)(2,1)}) %all-gather.32.cloned.1.call-update) | async-done | bytes 25165840 | tf_op jit(solution)/shard_map/all_gather | solution.py:194
  1044.1 16.8 multiply_convert_fusion.1
  1060.9 14.7 fusion.90
  1075.6 14.7 multiply_reduce_fusion.1
  1102.2 63.8 %while.31 = (s32[]{:T(128)}, f32[8,128,2,128]{1,3,2,0:T(8,128)}, bf16[8,512,128]{1,2,0:T(8,128)(2,1)}, bf16[8,512,128]{1,2,0:T(8,128)(2,1)}, bf16[8,512,128]{2,1...) while((s32[]{:T(128)}, f32[8,128,2,128]{1,3,2,0:T(8,128)}, ...), condition=%wide.region_13.14_spmd.clone.clone, body=%wide.region_11.13_spmd.clone.sunk.clone | while | flops 169312000 | bytes 5779593 | solution.py:225
  1180.3 18.7 reduce-scatter.7.cloned.1.call-done
  1200.9 29.5 %reduce-scatter.9.cloned.1.call-done = bf16[128,1024]{1,0:T(8,128)(2,1)} async-done(((bf16[512,1024]{1,0:T(8,128)(2,1)}), bf16[128,1024]{1,0:T(8,128)(2,1)}) %reduce-scatter.9.cloned.1.call-update) | async-done | bytes 262160
  1265.2 23.5 all-to-all-done.3
  1300.5 25.4 all-gather.40.cloned.1.call-done
  1334.6 49.5 %all-gather.34.cloned.1.call-done = bf16[512,4096]{0,1:T(8,128)(2,1)} async-done(((bf16[128,4096]{0,1:T(8,128)(2,1)}), bf16[512,4096]{0,1:T(8,128)(2,1)}) %all-gather.34.cloned.1.call-update) | async-done | bytes 4194320 | tf_op jit(solution)/shard_map/all_gather | solution.py:268
  1390.7 118.1 %all-gather.36.cloned.1.call-done = bf16[512,12288]{1,0:T(8,128)(2,1)} async-done(((bf16[128,12288]{1,0:T(8,128)(2,1)}), bf16[512,12288]{1,0:T(8,128)(2,1)}) %all-gather.36.cloned.1.call-update) | async-done | bytes 12582928 | tf_op jit(solution)/shard_map/all_gather | solution.py:269
  1550.7 41.2 %all-reduce = (f32[2048]{0:T(1024)}, f32[128]{0:T(128)}, f32[128]{0:T(128)}, f32[2048]{0:T(1024)}) all-reduce(f32[2048]{0:T(1024)S(1)} %get-tuple-element.250, f32[128]{0:T(128)S(1)} %get-tuple-element.246, f32[128]{0:T(128)S(1)} %get-tuple-element.252, ...), channel_id=1, replica_groups=mesh['shard'=4,'rep'=8] {'shard','rep'}, use_global_device_ids=true, to_apply=%region_20.21 | all-reduce | flops 4352 | bytes 34816 | tf_op jit(solution)/shard_map/psum | solution.py:257
  1594.8 94.1 %all-reduce.4.cloned.1.call-done = (bf16[512,2048]{1,0:T(8,128)(2,1)}, bf16[1536,2048]{1,0:T(8,128)(2,1)}) async-done(((bf16[512,2048]{1,0:T(8,128)(2,1)}, bf16[1536,2048]{1,0:T(8,128)(2,1)}), (bf16[512,2048]{1,0:T(8,128)(2,1)}, bf16[1536,2048]{1,0:T(8,128)(2,1)})) %all-reduce.4.cloned.1.call-update) | async-done | bytes 8388624 | tf_op jit(solution)/shard_map/psum | solution.py:279
  1701.7 1103.4 %all-gather.38.cloned.1.call-done = bf16[8,512,16384]{2,1,0:T(8,128)(2,1)} async-done(((bf16[1,512,16384]{2,1,0:T(8,128)(2,1)}), bf16[8,512,16384]{2,1,0:T(8,128)(2,1)}) %all-gather.38.cloned.1.call-update) | async-done | bytes 134217744 | tf_op jit(solution)/shard_map/all_gather | solution.py:15
  2805.1 50.0 %reduce_sum.147 = bf16[512,16384]{1,0:T(8,128)(2,1)} reduce(bf16[8,512,16384]{2,1,0:T(8,128)(2,1)} %all-gather.38.cloned.1.call-done, bf16[]{:T(256)} %constant.94.clone.1), dimensions={0}, to_apply=%region_21.22 | reduce | flops 58720256 | bytes 150994944 | tf_op jit(solution)/shard_map/reduce_sum | solution.py:15
  (288 shorter events, 328.4 us)
Async XLA Ops:
  7.2 58.0 %all-gather.20.cloned.1.call-start = ((), (), s32[]{:S(2)}) async-start(), calls=%async_computation.8 | async-start | bytes 5242880 | tf_op jit(solution)/shard_map/all_gather | solution.py:157
  7.9 111.7 %all-gather.16.cloned.1.call-start = ((), (), s32[]{:S(2)}) async-start(), calls=%async_computation.6 | async-start | bytes 5242880 | tf_op jit(solution)/shard_map/all_gather | solution.py:158
  8.7 139.7 %all-gather.22.cloned.1.call-start = ((), (), s32[]{:S(2)}) async-start(), calls=%async_computation.9 | async-start | bytes 1310720 | tf_op jit(solution)/shard_map/all_gather | solution.py:177
  77.1 160.5 %all-gather.24.cloned.1.call-start = ((), (), s32[]{:S(2)}) async-start(), calls=%async_computation.10 | async-start | bytes 10485760 | tf_op jit(solution)/shard_map/all_gather | solution.py:156
  77.7 188.7 %all-gather.18.cloned.1.call-start = ((), (), s32[]{:S(2)}) async-start(), calls=%async_computation.7 | async-start | bytes 1310720 | tf_op jit(solution)/shard_map/all_gather | solution.py:178
  123.3 232.3 %all-gather.26.cloned.1.call-start = ((), (), s32[]{:S(2)}) async-start(), calls=%async_computation.11 | async-start | bytes 10485760 | tf_op jit(solution)/shard_map/all_gather | solution.py:159
  123.9 461.2 %all-gather.28.cloned.1.call-start = ((), (), s32[]{:S(2)}) async-start(), calls=%async_computation.12 | async-start | bytes 31457280 | tf_op jit(solution)/shard_map/all_gather | solution.py:192
  124.7 689.9 %all-gather.30.cloned.1.call-start = ((), (), s32[]{:S(2)}) async-start(), calls=%async_computation.13 | async-start | bytes 31457280 | tf_op jit(solution)/shard_map/all_gather | solution.py:193
  125.4 918.6 %all-gather.32.cloned.1.call-start = ((), (), s32[]{:S(2)}) async-start(), calls=%async_computation.14 | async-start | bytes 31457280 | tf_op jit(solution)/shard_map/all_gather | solution.py:194
  126.2 1072.8 %reduce-scatter.7.cloned.1.call-start = ((), (), s32[]{:S(2)}) async-start(), calls=%async_computation.20 | async-start | bytes 1310720
  291.9 63.7 %copy-start.7 = (bf16[8,512,128]{2,1,0:T(8,128)(2,1)}, bf16[8,512,128]{2,1,0:T(8,128)(2,1)S(1)}, u32[]{:S(2)}) copy-start(bf16[8,512,128]{2,1,0:T(8,128)(2,1)S(1)} %get-tuple-element.611) | copy-start | bytes 3145732
  360.8 453.8 %copy-start.4 = (bf16[128,2048]{1,0:T(8,128)(2,1)}, bf16[128,2048]{1,0:T(8,128)(2,1)S(1)}, u32[]{:S(2)}) copy-start(bf16[128,2048]{1,0:T(8,128)(2,1)S(1)} %multiply_convert_fusion.5) | copy-start | bytes 1572868
  1170.9 59.5 %reduce-scatter.9.cloned.1.call-start = ((), (), s32[]{:S(2)}) async-start(), calls=%async_computation.21 | async-start | bytes 1310720
  1175.9 116.4 %all-gather.42.cloned.1.call-start = ((), (), s32[]{:S(2)}) async-start(), calls=%async_computation.19 | async-start | bytes 2621440 | tf_op jit(solution)/shard_map/all_gather | solution.py:271
  1176.5 149.5 %all-gather.40.cloned.1.call-start = ((), (), s32[]{:S(2)}) async-start(), calls=%async_computation.18 | async-start | bytes 2621440 | tf_op jit(solution)/shard_map/all_gather | solution.py:270
  1177.2 206.9 %all-gather.34.cloned.1.call-start = ((), (), s32[]{:S(2)}) async-start(), calls=%async_computation.15 | async-start | bytes 5242880 | tf_op jit(solution)/shard_map/all_gather | solution.py:268
  1178.8 53.9 %copy-start.9 = (f32[128,8,128]{0,2,1:T(8,128)S(1)}, f32[128,8,128]{0,2,1:T(8,128)}, u32[]{:S(2)}) copy-start(f32[128,8,128]{0,2,1:T(8,128)} %copy-done.8) | copy-start | bytes 1572868
  1234.1 274.6 %all-gather.36.cloned.1.call-start = ((), (), s32[]{:S(2)}) async-start(), calls=%async_computation.16 | async-start | bytes 15728640 | tf_op jit(solution)/shard_map/all_gather | solution.py:269
  1238.0 15.8 all-to-all-start.2
  1253.8 34.9 %all-to-all-start.3 = ((bf16[128,4,1536]{2,0,1:T(8,128)(2,1)}), bf16[128,4,1536]{2,0,1:T(8,128)(2,1)}, u32[]{:S(2)}, u32[]{:S(2)}) async-start(bf16[128,4,1536]{2,0,1:T(8,128)(2,1)} %bitcast.335), calls=%async_computation.3 | async-start | bytes 3145728 | tf_op jit(solution)/shard_map/all_to_all | solution.py:266
  1288.7 41.6 %all-to-all-start = ((bf16[128,4,512]{2,0,1:T(8,128)(2,1)}), bf16[128,4,512]{2,0,1:T(8,128)(2,1)S(1)}, u32[]{:S(2)}, u32[]{:S(2)}) async-start(bf16[128,4,512]{2,0,1:T(8,128)(2,1)} %fusion.58), calls=%async_computation | async-start | bytes 1048576 | tf_op jit(solution)/shard_map/all_to_all | solution.py:263
  1292.2 396.6 %all-reduce.4.cloned.1.call-start = ((), (), s32[]{:S(2)}) async-start(), calls=%async_computation.22 | async-start | bytes 16777216 | tf_op jit(solution)/shard_map/psum | solution.py:279
  1330.4 60.4 %all-to-all-start.1 = ((bf16[128,4,512]{2,0,1:T(8,128)(2,1)}), bf16[128,4,512]{2,0,1:T(8,128)(2,1)}, u32[]{:S(2)}, u32[]{:S(2)}) async-start(bf16[128,4,512]{2,0,1:T(8,128)(2,1)} %bitcast.264), calls=%async_computation.1 | async-start | bytes 1048576 | tf_op jit(solution)/shard_map/all_to_all | solution.py:264
  1334.5 1470.6 %all-gather.38.cloned.1.call-start = ((), (), s32[]{:S(2)}) async-start(), calls=%async_computation.17 | async-start | bytes 150994944 | tf_op jit(solution)/shard_map/all_gather | solution.py:15
  (17 other events, 239.2 us)
Sparse Core Ops, SparseCore 0:
  9.8 55.2 all-gather.19
  67.0 52.5 all-gather.15
  122.0 26.3 all-gather.21
  150.1 87.4 all-gather.23
  239.9 26.4 all-gather.17
  268.1 87.4 all-gather.25
  357.5 227.5 all-gather.27
  587.0 227.5 all-gather.29
  816.5 227.5 all-gather.31
  1171.0 27.9 reduce-scatter.6
  1202.5 27.9 reduce-scatter.8
  1232.1 56.7 all-gather.41
  1290.8 35.1 all-gather.39
  1328.2 55.8 all-gather.33
  1386.4 122.3 all-gather.35
  1512.2 176.5 all-reduce.3
  1690.3 1114.8 all-gather.37
